TPU v7x, 256 devices: a whole 4x4x8 slice. The times are simulated.
256 devices in a mesh: gx: 8 (over z), gy: 8 (over x, y_lo), gz: 4 (over y_hi, core).
Axes of the slice: x: 4, y: 4 (y_hi: 2, y_lo: 2; y = y_hi * 2 + y_lo), z: 8, core: 2. Of those that a mesh axis runs over, the one named last changes fastest.
Arguments:
- fields_now: float32 [24, 64, 64, 512], P(None, 'gx', 'gy', 'gz'), may hold values from -6 to 6
- parent: float32 [24, 64, 64, 512], P(None, 'gx', 'gy', 'gz'), may hold values from -6 to 6
- advect: float32 [3, 24, 24], replicated, may hold values from -0.75 to 0.75
- diffuse: float32 [3, 24, 24], replicated, may hold values from -0.25 to 0.25
- box_shift: int32 [3], replicated, may hold values from 1 to 4
Outputs:
- section_slope: float32 [24, 64, 64, 512], P(None, 'gx', 'gy', 'gz')
- section_value: float32 [24, 64, 64, 512], P(None, 'gx', 'gy', 'gz')
All inputs are finite; a program needn't handle non-finite values.
Results may differ from a plain program's by a relative error of at most 0.0001.
Values sent between devices are 32-bit elements; how exact they have to be, the bound alone decides.
A program may use at most 64 MiB of HBM per device.

v0:
```python
import jax
import jax.numpy as jnp
from jax import lax
from jax.sharding import PartitionSpec as P

dissipation = 1.0
half_step = 0.125


def shifted(value, axis, by):
    devices = lax.axis_size(axis)
    pairs = [(i, i + by) for i in range(devices) if 0 <= i + by < devices]
    return lax.ppermute(value, axis, pairs)


def extended_2(value, sides, width):
    edges = {}
    for axis, dim in sides:
        devices, length = (lax.axis_size(axis), value.shape[dim])
        up = [(i, (i + 1) % devices) for i in range(devices - 1)]
        last = lax.slice_in_dim(value, length - width, length, axis=dim)
        initial = lax.slice_in_dim(value, 0, width, axis=dim)
        edges[dim] = (
            lax.ppermute(last, axis, up),
            lax.ppermute(initial, axis, [(b, a) for a, b in up]),
        )
    done = []
    for _, dim in sides:
        low, high = edges[dim]
        around = [(width, width) if d in done else (0, 0) for d in range(value.ndim)]
        value = jnp.concatenate([jnp.pad(low, around), value, jnp.pad(high, around)], axis=dim)
        done.append(dim)
    return value


def line_terms(padded_line, axis):
    length = padded_line.shape[axis] - 6

    def take_at(offset):
        return lax.slice_in_dim(padded_line, 3 + offset, 3 + offset + length, axis=axis)

    first_diff = (take_at(-2) - 8.0 * take_at(-1) + 8.0 * take_at(1) - take_at(2)) / 12.0
    second_diff = (
        -take_at(-2) + 16.0 * take_at(-1) - 30.0 * take_at(0) + 16.0 * take_at(1) - take_at(2)
    ) / 12.0
    sixth_diff = (
        take_at(-3)
        - 6.0 * take_at(-2)
        + 15.0 * take_at(-1)
        - 20.0 * take_at(0)
        + 15.0 * take_at(1)
        - 6.0 * take_at(2)
        + take_at(3)
    )
    return (first_diff, second_diff, sixth_diff)


def mix_fields(matrix, field):
    flat = field.reshape(field.shape[0], -1)
    return jnp.dot(
        matrix, flat, precision=lax.Precision.HIGHEST, preferred_element_type=jnp.float32
    ).reshape(field.shape)


def center_crop(padded, axis):
    window = [slice(None)] * 4
    for other in (1, 2, 3):
        if other != axis:
            window[other] = slice(3, padded.shape[other] - 3)
    return padded[tuple(window)]


def axis_terms(line, axis, advect, diffuse):
    first_diff, second_diff, sixth_diff = line_terms(line, axis)
    coupled = mix_fields(advect[axis - 1], first_diff) + mix_fields(diffuse[axis - 1], second_diff)
    return (coupled, sixth_diff)


def whole_terms(padded, advect, diffuse):
    linear, smooth = axis_terms(center_crop(padded, 1), 1, advect, diffuse)
    for axis in (2, 3):
        coupled, sixth_diff = axis_terms(center_crop(padded, axis), axis, advect, diffuse)
        linear = linear + coupled
        smooth = smooth + sixth_diff
    return (linear, smooth)


def finish(new_box, linear, smooth):
    lapse_factor = 1.0 + 0.25 * jnp.tanh(new_box[0])
    section_slope = lapse_factor * linear + dissipation / 64.0 * smooth
    section_value = new_box + half_step * section_slope
    return (section_slope, section_value)


def box_cells(lengths, block, offset):
    rows_x = (
        lax.axis_index("gx") * block[0]
        - offset
        + lax.broadcasted_iota(jnp.int32, (1, lengths[0], 1, 1), 1)
    )
    rows_y = (
        lax.axis_index("gy") * block[1]
        - offset
        + lax.broadcasted_iota(jnp.int32, (1, 1, lengths[1], 1), 2)
    )
    rows_z = (
        lax.axis_index("gz") * block[2]
        - offset
        + lax.broadcasted_iota(jnp.int32, (1, 1, 1, lengths[2]), 3)
    )
    totals = (
        block[0] * lax.axis_size("gx"),
        block[1] * lax.axis_size("gy"),
        block[2] * lax.axis_size("gz"),
    )
    return ((rows_x, rows_y, rows_z), totals)


def from_old_mask(cells, totals, box_shift):
    return (
        (cells[0] + box_shift[0] < totals[0])
        & (cells[1] + box_shift[1] < totals[1])
        & (cells[2] + box_shift[2] < totals[2])
    )


def local(fields_now, parent, advect, diffuse, box_shift):
    count_f, count_x, count_y, count_z = fields_now.shape
    block = (count_x, count_y, count_z)
    anchor = jnp.zeros((), jnp.int32)
    from_above = shifted(fields_now[:, :4], "gx", -1)
    extended = jnp.concatenate([fields_now, from_above], axis=1)
    from_above = shifted(extended[:, :, :4], "gy", -1)
    extended = jnp.concatenate([extended, from_above], axis=2)
    from_above = shifted(extended[:, :, :, :4], "gz", -1)
    extended = jnp.concatenate([extended, from_above], axis=3)
    moved_cells = lax.dynamic_slice(
        extended, (anchor, box_shift[0], box_shift[1], box_shift[2]), fields_now.shape
    )
    cells, totals = box_cells(block, block, 0)
    new_box = jnp.where(from_old_mask(cells, totals, box_shift), moved_cells, parent)
    padded = extended_2(new_box, (("gx", 1), ("gy", 2), ("gz", 3)), 3)
    linear, smooth = whole_terms(padded, advect, diffuse)
    return finish(new_box, linear, smooth)


def solution(mesh):
    return jax.shard_map(
        local,
        mesh=mesh,
        in_specs=(P(None, "gx", "gy", "gz"), P(None, "gx", "gy", "gz"), P(), P(), P()),
        out_specs=(P(None, "gx", "gy", "gz"), P(None, "gx", "gy", "gz")),
        check_vma=False,
    )
```

profile of v0, /device:TPU:111, one launch (start us, length us, event | category | flops | bytes accessed | tf_op | source)
XLA Modules:
  0.0 102.2 jit_solution(10155979678736009524)
XLA Ops:
  2.0 1.9 %collective-permute-start = (f32[24,4,8,128]{3,0,2,1:T(8,128)S(1)}, f32[24,4,8,128]{3,0,2,1:T(8,128)S(1)}, u32[]{:S(2)}, u32[]{:S(2)}) collective-permute-start(f32[24,4,8,128]{3,0,2,1:T(8,128)S(1)} %copy.81), channel_id=1, source_target_pairs={{32,0},{64,32},{96,64},{128,96},{160,128},{192,160},{224,192},{33,... | collective-permute-start | bytes 1179656 | tf_op jit(solution)/shard_map/ppermute | solution.py:13
  4.4 11.1 %collective-permute-done = f32[24,4,8,128]{3,0,2,1:T(8,128)S(1)} collective-permute-done((f32[24,4,8,128]{3,0,2,1:T(8,128)S(1)}, f32[24,4,8,128]{3,0,2,1:T(8,128)S(1)}, u32[]{:S(2)}, u32[]{:S(2)}) %collective-permute-start) | collective-permute-done | bytes 393248 | tf_op jit(solution)/shard_map/ppermute | solution.py:13
  15.5 2.1 %collective-permute-start.1 = (f32[24,12,4,128]{3,0,2,1:T(8,128)S(1)}, f32[24,12,4,128]{3,0,2,1:T(8,128)S(1)}, u32[]{:S(2)}, u32[]{:S(2)}) collective-permute-start(f32[24,12,4,128]{3,0,2,1:T(8,128)S(1)} %slice.217), channel_id=1, source_target_pairs={{4,0},{8,4},{12,8},{16,12},{20,16},{24,20},{28,24},{5,1},{9,5},{13... | collective-permute-start | bytes 1769480 | tf_op jit(solution)/shard_map/ppermute | solution.py:13
  18.9 1.3 %add_compare_fusion.1 = (pred[8]{0:T(512)(128)(4,1)S(1)}, pred[8]{0:T(512)(128)(4,1)S(1)}) fusion(s32[]{:T(128)} %bitcast.1, s32[]{:T(128)S(6)} %mul.121, s32[]{:T(128)} %bitcast, s32[]{:T(128)S(6)} %mul.120), kind=kLoop, calls=%fused_computation.98 | loop fusion | flops 48 | bytes 32 | tf_op jit(solution)/shard_map/lt | solution.py:122
  20.3 8.7 %collective-permute-done.1 = f32[24,12,4,128]{3,0,2,1:T(8,128)S(1)} collective-permute-done((f32[24,12,4,128]{3,0,2,1:T(8,128)S(1)}, f32[24,12,4,128]{3,0,2,1:T(8,128)S(1)}, u32[]{:S(2)}, u32[]{:S(2)}) %collective-permute-start.1) | collective-permute-done | bytes 589856 | tf_op jit(solution)/shard_map/ppermute | solution.py:13
  28.9 1.4 %pad_maximum_fusion.1 = f32[24,12,12,4]{3,0,2,1:T(8,128)} fusion(f32[24,12,4,128]{3,0,2,1:T(8,128)S(1)} %collective-permute-done.1, f32[24,12,8,128]{3,0,2,1:T(8,128)S(1)} %constant_dynamic-update-slice_fusion), kind=kLoop, calls=%fused_computation.14 | loop fusion | flops 13824 | bytes 1824768 | tf_op jit(solution)/shard_map/concatenate | solution.py:134
  30.3 2.8 %copy.25 = f32[24,12,12,4]{0,2,3,1:T(8,128)S(1)} copy(f32[24,12,12,4]{3,0,2,1:T(8,128)} %pad_maximum_fusion.1) | data formatting | bytes 110592 | tf_op jit(solution)/shard_map/slice | solution.py:135
  33.1 4.1 %collective-permute-start.2 = (f32[24,12,12,4]{0,2,3,1:T(8,128)S(1)}, f32[24,12,12,4]{0,2,3,1:T(8,128)S(1)}, u32[]{:S(2)}, u32[]{:S(2)}) collective-permute-start(f32[24,12,12,4]{0,2,3,1:T(8,128)S(1)} %copy.25), channel_id=1, source_target_pairs={{1,0},{2,1},{3,2},{5,4},{6,5},{7,6},{9,8},{10,9},{11,10},{13,12},{... | collective-permute-start | bytes 165896 | tf_op jit(solution)/shard_map/ppermute | solution.py:13
  43.1 1.8 %collective-permute-done.2 = f32[24,12,12,4]{0,2,3,1:T(8,128)S(1)} collective-permute-done((f32[24,12,12,4]{0,2,3,1:T(8,128)S(1)}, f32[24,12,12,4]{0,2,3,1:T(8,128)S(1)}, u32[]{:S(2)}, u32[]{:S(2)}) %collective-permute-start.2) | collective-permute-done | bytes 55328 | tf_op jit(solution)/shard_map/ppermute | solution.py:13
  44.9 2.1 %copy.26 = f32[24,12,12,4]{3,0,2,1:T(8,128)} copy(f32[24,12,12,4]{0,2,3,1:T(8,128)S(1)} %collective-permute-done.2) | data formatting | bytes 110592 | tf_op jit(solution)/shard_map/ppermute | solution.py:13
  47.1 1.9 %fusion.9 = f32[24,8,8,128]{3,0,2,1:T(8,128)S(1)} fusion(s32[]{:T(128)S(6)} %select_n.13, s32[]{:T(128)S(6)} %select_n.14, s32[]{:T(128)S(6)} %select_n.15, f32[24,12,8,128]{3,0,2,1:T(8,128)S(1)} %constant_dynamic-update-slice_fusion, f32[24,12,4,128]{3,0,2,1:T(8,128)S(1)} %collective-permute-done.1, f32[24,12,12,4]{3,0,2,1:T(8,128)} %copy.26, ...), kind=kLoop, calls=%fused_computation.30 | loop fusion | flops 589824 | bytes 3405836 | tf_op jit(solution)/shard_map/jit(_where)/select_n | solution.py:141
  50.0 4.7 %collective-permute-start.6 = (f32[24,8,3,128]{3,1,2,0:T(8,128)S(1)}, f32[24,8,3,128]{3,1,2,0:T(8,128)S(1)}, u32[]{:S(2)}, u32[]{:S(2)}) collective-permute-start(f32[24,8,3,128]{3,1,2,0:T(8,128)S(1)} %copy.32), channel_id=1, source_target_pairs={{4,0},{8,4},{12,8},{16,12},{20,16},{24,20},{28,24},{5,1},{9,5},{13... | collective-permute-start | bytes 884744 | tf_op jit(solution)/shard_map/ppermute | solution.py:25
  54.7 1.9 %collective-permute-start.4 = (f32[24,3,8,128]{3,0,2,1:T(8,128)}, f32[24,3,8,128]{3,0,2,1:T(8,128)S(1)}, u32[]{:S(2)}, u32[]{:S(2)}) collective-permute-start(f32[24,3,8,128]{3,0,2,1:T(8,128)} %get-tuple-element.25), channel_id=1, source_target_pairs={{32,0},{64,32},{96,64},{128,96},{160,128},{192,160},{224,192},{33,... | collective-permute-start | bytes 884744 | tf_op jit(solution)/shard_map/ppermute | solution.py:25
  56.6 4.6 %collective-permute-start.3 = (f32[24,3,8,128]{3,0,2,1:T(8,128)}, f32[24,3,8,128]{3,0,2,1:T(8,128)S(1)}, u32[]{:S(2)}, u32[]{:S(2)}) collective-permute-start(f32[24,3,8,128]{3,0,2,1:T(8,128)} %get-tuple-element.24), channel_id=1, source_target_pairs={{0,32},{32,64},{64,96},{96,128},{128,160},{160,192},{192,224},{1,3... | collective-permute-start | bytes 884744 | tf_op jit(solution)/shard_map/ppermute | solution.py:24
  62.0 1.3 %collective-permute-start.5 = (f32[24,8,3,128]{3,1,2,0:T(8,128)}, f32[24,8,3,128]{3,1,2,0:T(8,128)}, u32[]{:S(2)}, u32[]{:S(2)}) collective-permute-start(f32[24,8,3,128]{3,1,2,0:T(8,128)} %copy.30), channel_id=1, source_target_pairs={{0,4},{4,8},{8,12},{12,16},{16,20},{20,24},{24,28},{1,5},{5,9},{9,... | collective-permute-start | bytes 884744 | tf_op jit(solution)/shard_map/ppermute | solution.py:24
  64.6 2.5 %collective-permute-start.7 = (f32[24,8,8,3]{0,2,3,1:T(8,128)}, f32[24,8,8,3]{0,2,3,1:T(8,128)S(1)}, u32[]{:S(2)}, u32[]{:S(2)}) collective-permute-start(f32[24,8,8,3]{0,2,3,1:T(8,128)} %copy.36), channel_id=1, source_target_pairs={{0,1},{1,2},{2,3},{4,5},{5,6},{6,7},{8,9},{9,10},{10,11},{12,13},{... | collective-permute-start | bytes 55304 | tf_op jit(solution)/shard_map/ppermute | solution.py:24
  67.6 6.1 %collective-permute-done.7 = f32[24,8,8,3]{0,2,3,1:T(8,128)S(1)} collective-permute-done((f32[24,8,8,3]{0,2,3,1:T(8,128)}, f32[24,8,8,3]{0,2,3,1:T(8,128)S(1)}, u32[]{:S(2)}, u32[]{:S(2)}) %collective-permute-start.7) | collective-permute-done | bytes 18464 | tf_op jit(solution)/shard_map/ppermute | solution.py:24
  73.7 1.9 %collective-permute-start.8 = (f32[24,8,8,3]{0,2,3,1:T(8,128)S(1)}, f32[24,8,8,3]{0,2,3,1:T(8,128)}, u32[]{:S(2)}, u32[]{:S(2)}) collective-permute-start(f32[24,8,8,3]{0,2,3,1:T(8,128)S(1)} %copy.38), channel_id=1, source_target_pairs={{1,0},{2,1},{3,2},{5,4},{6,5},{7,6},{9,8},{10,9},{11,10},{13,12},{... | collective-permute-start | bytes 55304 | tf_op jit(solution)/shard_map/ppermute | solution.py:25
  76.7 5.1 %collective-permute-done.8 = f32[24,8,8,3]{0,2,3,1:T(8,128)} collective-permute-done((f32[24,8,8,3]{0,2,3,1:T(8,128)S(1)}, f32[24,8,8,3]{0,2,3,1:T(8,128)}, u32[]{:S(2)}, u32[]{:S(2)}) %collective-permute-start.8) | collective-permute-done | bytes 18464 | tf_op jit(solution)/shard_map/ppermute | solution.py:25
  81.9 1.3 %copy.39 = f32[24,8,8,3]{3,0,2,1:T(8,128)S(1)} copy(f32[24,8,8,3]{0,2,3,1:T(8,128)} %collective-permute-done.8) | data formatting | bytes 36864 | tf_op jit(solution)/shard_map/ppermute | solution.py:25
  84.4 3.0 %select_maximum_fusion.1 = (f32[24,14,14,131]{3,0,2,1:T(8,128)S(1)}, f32[24,14,14,131]{3,0,2,1:T(8,128)S(1)}) fusion(f32[24,8,8,3]{3,0,2,1:T(8,128)S(1)} %copy.37, f32[24,14,3,128]{3,0,2,1:T(8,128)S(1)} %pad.15, f32[24,3,8,128]{3,0,2,1:T(8,128)S(1)} %collective-permute-done.4, f32[24,8,8,128]{3,0,2,1:T(8,128)S(1)} %fusion.9, ...), kind=kLoop, calls=%fused_computation.7 | loop fusion | flops 8627136 | bytes 7375104 | tf_op jit(solution)/shard_map/concatenate | solution.py:31
  95.5 1.3 %fusion.1 = f32[8192,24]{0,1:T(8,128)S(1)} fusion(f32[8192,24]{0,1:T(8,128)S(1)} %convolution_add_fusion.2, f32[8192,24]{0,1:T(8,128)S(1)} %fusion.17, f32[3,8,64,128]{3,2,1,0:T(8,128)S(1)} %bitcast.62, f32[3,24,24]{2,1,0:T(8,128)S(1)} %copy-done.4), kind=kOutput, calls=%fused_computation.3 | convolution fusion | flops 57016320 | bytes 3158016 | tf_op jit(solution)/shard_map/dot_general | solution.py:60
  96.8 1.3 %fusion.2 = f32[3,8,64,128]{3,1,2,0:T(8,128)S(1)} fusion(f32[8192,24]{0,1:T(8,128)S(1)} %fusion.1, f32[8192,24]{0,1:T(8,128)S(1)} %fusion.12, f32[3,8,64,128]{3,2,1,0:T(8,128)S(1)} %bitcast.63, f32[3,24,24]{2,1,0:T(8,128)S(1)} %copy-done.4), kind=kOutput, calls=%fused_computation.19 | convolution fusion | flops 57016320 | bytes 3158016 | tf_op jit(solution)/shard_map/dot_general | solution.py:60
  98.2 1.9 %multiply_add_fusion = (f32[24,8,8,128]{3,0,2,1:T(8,128)S(1)}, f32[24,8,8,128]{3,0,2,1:T(8,128)S(1)}) fusion(f32[24,8,8,128]{3,0,2,1:T(8,128)S(1)} %fusion.9, f32[24,14,14,131]{3,0,2,1:T(8,128)S(1)} %get-tuple-element.13, f32[24,14,14,131]{3,0,2,1:T(8,128)S(1)} %get-tuple-element.12, f32[24,14,11,128]{3,0,2,1:T(8,128)S(1)} %get-tuple-element.17, ...), kind=kLoop, calls=%fused_computation.71 | loop fusion | flops 8650752 | bytes 13205504 | tf_op jit(solution)/shard_map/add | solution.py:91
  (54 shorter events, 19.2 us)
Async XLA Ops:
  0.6 3.3 %copy-start = (f32[24,8,8,128]{3,2,1,0:T(8,128)S(1)}, f32[24,8,8,128]{3,2,1,0:T(8,128)}, u32[]{:S(2)}) copy-start(f32[24,8,8,128]{3,2,1,0:T(8,128)} %param.5) | copy-start | bytes 2359300
  2.0 15.7 %copy-start.5 = (s32[3]{0:T(128)S(1)}, s32[3]{0:T(128)}, u32[]{:S(2)}) copy-start(s32[3]{0:T(128)} %param.9) | copy-start | bytes 40
  2.0 13.5 %collective-permute-start = (f32[24,4,8,128]{3,0,2,1:T(8,128)S(1)}, f32[24,4,8,128]{3,0,2,1:T(8,128)S(1)}, u32[]{:S(2)}, u32[]{:S(2)}) collective-permute-start(f32[24,4,8,128]{3,0,2,1:T(8,128)S(1)} %copy.81), channel_id=1, source_target_pairs={{32,0},{64,32},{96,64},{128,96},{160,128},{192,160},{224,192},{33,... | collective-permute-start | bytes 1179656 | tf_op jit(solution)/shard_map/ppermute | solution.py:13
  15.5 13.4 %collective-permute-start.1 = (f32[24,12,4,128]{3,0,2,1:T(8,128)S(1)}, f32[24,12,4,128]{3,0,2,1:T(8,128)S(1)}, u32[]{:S(2)}, u32[]{:S(2)}) collective-permute-start(f32[24,12,4,128]{3,0,2,1:T(8,128)S(1)} %slice.217), channel_id=1, source_target_pairs={{4,0},{8,4},{12,8},{16,12},{20,16},{24,20},{28,24},{5,1},{9,5},{13... | collective-permute-start | bytes 1769480 | tf_op jit(solution)/shard_map/ppermute | solution.py:13
  30.3 16.8 %copy-start.1 = (f32[24,8,8,128]{3,2,1,0:T(8,128)S(1)}, f32[24,8,8,128]{3,2,1,0:T(8,128)}, u32[]{:S(2)}) copy-start(f32[24,8,8,128]{3,2,1,0:T(8,128)} %param.6) | copy-start | bytes 2359300
  33.1 11.8 %collective-permute-start.2 = (f32[24,12,12,4]{0,2,3,1:T(8,128)S(1)}, f32[24,12,12,4]{0,2,3,1:T(8,128)S(1)}, u32[]{:S(2)}, u32[]{:S(2)}) collective-permute-start(f32[24,12,12,4]{0,2,3,1:T(8,128)S(1)} %copy.25), channel_id=1, source_target_pairs={{1,0},{2,1},{3,2},{5,4},{6,5},{7,6},{9,8},{10,9},{11,10},{13,12},{... | collective-permute-start | bytes 165896 | tf_op jit(solution)/shard_map/ppermute | solution.py:13
  50.0 33.2 %collective-permute-start.6 = (f32[24,8,3,128]{3,1,2,0:T(8,128)S(1)}, f32[24,8,3,128]{3,1,2,0:T(8,128)S(1)}, u32[]{:S(2)}, u32[]{:S(2)}) collective-permute-start(f32[24,8,3,128]{3,1,2,0:T(8,128)S(1)} %copy.32), channel_id=1, source_target_pairs={{4,0},{8,4},{12,8},{16,12},{20,16},{24,20},{28,24},{5,1},{9,5},{13... | collective-permute-start | bytes 884744 | tf_op jit(solution)/shard_map/ppermute | solution.py:25
  54.7 29.7 %collective-permute-start.4 = (f32[24,3,8,128]{3,0,2,1:T(8,128)}, f32[24,3,8,128]{3,0,2,1:T(8,128)S(1)}, u32[]{:S(2)}, u32[]{:S(2)}) collective-permute-start(f32[24,3,8,128]{3,0,2,1:T(8,128)} %get-tuple-element.25), channel_id=1, source_target_pairs={{32,0},{64,32},{96,64},{128,96},{160,128},{192,160},{224,192},{33,... | collective-permute-start | bytes 884744 | tf_op jit(solution)/shard_map/ppermute | solution.py:25
  56.6 27.8 %collective-permute-start.3 = (f32[24,3,8,128]{3,0,2,1:T(8,128)}, f32[24,3,8,128]{3,0,2,1:T(8,128)S(1)}, u32[]{:S(2)}, u32[]{:S(2)}) collective-permute-start(f32[24,3,8,128]{3,0,2,1:T(8,128)} %get-tuple-element.24), channel_id=1, source_target_pairs={{0,32},{32,64},{64,96},{96,128},{128,160},{160,192},{192,224},{1,3... | collective-permute-start | bytes 884744 | tf_op jit(solution)/shard_map/ppermute | solution.py:24
  62.0 21.3 %collective-permute-start.5 = (f32[24,8,3,128]{3,1,2,0:T(8,128)}, f32[24,8,3,128]{3,1,2,0:T(8,128)}, u32[]{:S(2)}, u32[]{:S(2)}) collective-permute-start(f32[24,8,3,128]{3,1,2,0:T(8,128)} %copy.30), channel_id=1, source_target_pairs={{0,4},{4,8},{8,12},{12,16},{16,20},{20,24},{24,28},{1,5},{5,9},{9,... | collective-permute-start | bytes 884744 | tf_op jit(solution)/shard_map/ppermute | solution.py:24
  64.6 9.1 %collective-permute-start.7 = (f32[24,8,8,3]{0,2,3,1:T(8,128)}, f32[24,8,8,3]{0,2,3,1:T(8,128)S(1)}, u32[]{:S(2)}, u32[]{:S(2)}) collective-permute-start(f32[24,8,8,3]{0,2,3,1:T(8,128)} %copy.36), channel_id=1, source_target_pairs={{0,1},{1,2},{2,3},{4,5},{5,6},{6,7},{8,9},{9,10},{10,11},{12,13},{... | collective-permute-start | bytes 55304 | tf_op jit(solution)/shard_map/ppermute | solution.py:24
  73.7 8.2 %collective-permute-start.8 = (f32[24,8,8,3]{0,2,3,1:T(8,128)S(1)}, f32[24,8,8,3]{0,2,3,1:T(8,128)}, u32[]{:S(2)}, u32[]{:S(2)}) collective-permute-start(f32[24,8,8,3]{0,2,3,1:T(8,128)S(1)} %copy.38), channel_id=1, source_target_pairs={{1,0},{2,1},{3,2},{5,4},{6,5},{7,6},{9,8},{10,9},{11,10},{13,12},{... | collective-permute-start | bytes 55304 | tf_op jit(solution)/shard_map/ppermute | solution.py:25
  89.2 0.8 copy-start.3
  92.8 1.4 %copy-start.4 = (f32[3,24,24]{2,1,0:T(8,128)S(1)}, f32[3,24,24]{2,1,0:T(8,128)}, u32[]{:S(2)}) copy-start(f32[3,24,24]{2,1,0:T(8,128)} %param.8) | copy-start | bytes 20740
  96.8 1.4 %copy-start.2 = (f32[1,8,8,128]{3,0,2,1:T(1,128)S(1)}, f32[1,8,8,128]{3,0,2,1:T(1,128)}, u32[]{:S(2)}) copy-start(f32[1,8,8,128]{3,0,2,1:T(1,128)} %fusion.44) | copy-start | bytes 98308
where the time goes:
time: 103 us; the launch traced here: 102 us
  waiting for transfers between devices  32.7 us (32%)
  starting transfers between devices  25.1 us (24%)
  local copies, waits for them, and re-layouts  17.2 us (17%)
  other arithmetic  12.8 us (12%)
  matrix products  7.56 us (7%)
  between operations  6.8 us (7%)
    ppermute x3, waiting for transfers between devices, shifted(): return lax.ppermute(value, axis, pairs)  21.5 us
    ppermute x3, starting transfers between devices, extended_2(): lax.ppermute(initial, axis, [(b, a) for a, b in up])  8.56 us
    ppermute x3, starting transfers between devices, extended_2(): lax.ppermute(last, axis, up)  8.4 us
    ppermute x3, starting transfers between devices, shifted(): return lax.ppermute(value, axis, pairs)  8.15 us
    dot_general x6, matrix products, mix_fields(): jnp.dot(matrix, flat, precision=lax.Precision.HIGHEST, preferred_element_...  7.56 us
    ppermute x3, waiting for transfers between devices, extended_2(): lax.ppermute(last, axis, up)  6.07 us
    ppermute x3, waiting for transfers between devices, extended_2(): lax.ppermute(initial, axis, [(b, a) for a, b in up])  5.15 us
    concatenate x2, other arithmetic, extended_2(): jnp.concatenate([jnp.pad(low, around), value, jnp.pad(high, around)], axi...  3.23 us
  transfers between devices with their start and end apart: 9, of which 5 were waited for; matrix products, arithmetic and copies ran while one was open for 9% of the time, Pallas kernels for 0%

commit v1 on v0

v1 whole, which is shorter than its diff:
```python
import jax
import jax.numpy as jnp
from jax import lax
from jax.experimental import pallas as pl
from jax.experimental.pallas import tpu as pltpu
from jax.sharding import PartitionSpec as P

MESH = pl.DeviceIdType.MESH
F32, BF16 = jnp.float32, jnp.bfloat16
GROUPS = 3
NX, NY, NZ = 8, 8, 128


def lane_iota():
    return lax.broadcasted_iota(jnp.int32, (8, NZ), 1)


def kernel(shift, now_hbm, parent_hbm, advect, diffuse, slope_hbm, value_hbm, *scratch):
    scratch = list(scratch)

    def take(count):
        got = scratch[:count]
        del scratch[:count]
        return got

    now_v, parent_v, slope_v, value_v, acc, mixed, weights, weight_f32 = take(8)
    raw = [take(2) for _ in range(GROUPS)]
    moved = take(GROUPS)
    zs, zr = take(GROUPS), take(GROUPS)
    box = take(GROUPS)
    arm_sd, arm_su, arm_rd, arm_ru = take(GROUPS), take(GROUPS), take(GROUPS), take(GROUPS)
    load_sem, store_sem, a_send, a_recv, b_send, b_recv, z_send, z_recv, arm_send, arm_recv = take(10)

    gx, gy, gz = lax.axis_index("gx"), lax.axis_index("gy"), lax.axis_index("gz")
    ex, ey, ez = lax.axis_size("gx"), lax.axis_size("gy"), lax.axis_size("gz")
    place = {"gx": gx, "gy": gy, "gz": gz}
    has_low = {"gx": gx > 0, "gy": gy > 0, "gz": gz > 0}
    has_high = {"gx": gx < ex - 1, "gy": gy < ey - 1, "gz": gz < ez - 1}
    s0, s1, s2 = shift[0], shift[1], shift[2]

    def remote(src, dst, send, recv, axis, step):
        return pltpu.make_async_remote_copy(
            src_ref=src, dst_ref=dst, send_sem=send, recv_sem=recv,
            device_id={axis: place[axis] + step}, device_id_type=MESH)

    loads = [pltpu.make_async_copy(now_hbm.at[pl.ds(8 * c, 8)], now_v.at[pl.ds(8 * c, 8)], load_sem.at[c])
             for c in range(GROUPS)]
    loads.append(pltpu.make_async_copy(parent_hbm, parent_v, load_sem.at[GROUPS]))
    for load in loads:
        load.start()

    barrier = pltpu.get_barrier_semaphore()
    for axis in ("gx", "gy", "gz"):
        for present, step in ((has_low[axis], -1), (has_high[axis], 1)):
            @pl.when(present)
            def _():
                pl.semaphore_signal(barrier, inc=1, device_id={axis: place[axis] + step}, device_id_type=MESH)

    for c in range(GROUPS):
        loads[c].wait()
        for h in range(2):
            def turn(x, carry, c=c, h=h):
                raw[c][h][x, 0:8] = jnp.swapaxes(now_v[8 * c:8 * c + 8, 4 * h + x], 0, 1)
                return carry
            lax.fori_loop(0, 4, turn, 0)

    peers = [has[axis].astype(jnp.int32) for axis in ("gx", "gy", "gz") for has in (has_low, has_high)]
    pl.semaphore_wait(barrier, sum(peers))

    a_copies = [[remote(raw[c][h].at[:, 0:4], raw[c][h].at[:, 8:12], a_send.at[c, h], a_recv.at[c, h], "gy", -1)
                 for h in range(2)] for c in range(GROUPS)]
    b_copies = [remote(moved[c].at[0:4], moved[c].at[8:12], b_send.at[c], b_recv.at[c], "gx", -1) for c in range(GROUPS)]
    z_copies = [remote(zs[c], zr[c], z_send.at[c], z_recv.at[c], "gz", -1) for c in range(GROUPS)]

    @pl.when(has_low["gy"])
    def _():
        for h in range(2):
            for c in range(GROUPS):
                a_copies[c][h].start()

    edges = (
        ("gx", has_low, lambda r: r.at[0:3, 3:11]), ("gx", has_high, lambda r: r.at[11:14, 3:11]),
        ("gy", has_low, lambda r: r.at[3:11, 0:3]), ("gy", has_high, lambda r: r.at[3:11, 11:14]))
    for axis, has, view in edges:
        @pl.when(jnp.logical_not(has[axis]))
        def _():
            for c in range(GROUPS):
                ref = view(box[c])
                ref[...] = jnp.zeros(ref.shape, F32)

    @pl.when(jnp.logical_not(has_low["gz"]))
    def _():
        for c in range(GROUPS):
            arm_rd[c][...] = jnp.zeros(arm_rd[c].shape, F32)

    @pl.when(jnp.logical_not(has_high["gz"]))
    def _():
        for c in range(GROUPS):
            arm_ru[c][...] = jnp.zeros(arm_ru[c].shape, F32)

    for c in range(GROUPS):
        for k in range(12):
            q = k % 6
            source = advect if q < 3 else diffuse
            weight_f32[:, 8 * k:8 * k + 8] = source[q % 3, :, 8 * c:8 * c + 8] * (1.0 / 12.0)
        full = weight_f32[...]
        high = full.astype(BF16).astype(F32)
        weights[c] = jnp.concatenate([high, full - high], axis=0).astype(BF16)

    def shift_y(c, h):
        def body(x, carry):
            moved[c][4 * h + x] = raw[c][h][x, pl.ds(s1, 8)]
            return carry
        lax.fori_loop(0, 4, body, 0)

    for c in range(GROUPS):
        @pl.when(has_high["gy"])
        def _():
            a_copies[c][0].wait_recv()
        shift_y(c, 0)

        @pl.when(has_low["gx"])
        def _():
            b_copies[c].start()

    loads[GROUPS].wait()

    lane = lane_iota()
    group = lane // 4

    for c in range(GROUPS):
        @pl.when(has_high["gy"])
        def _():
            a_copies[c][1].wait_recv()
        shift_y(c, 1)

        @pl.when(has_high["gx"])
        def _():
            b_copies[c].wait_recv()

        for half in range(2):
            def pack(x, packed, c=c, half=half):
                for y in range(8):
                    tile = moved[c][4 * half + x + s0, y]
                    at = 8 * x + y
                    packed = jnp.where(group == at, pltpu.roll(tile, 4 * at, 1), packed)
                return packed
            zs[c][half] = lax.fori_loop(0, 4, pack, jnp.zeros((8, NZ), F32))

        @pl.when(has_low["gz"])
        def _():
            z_copies[c].start()

    def arm(c, k, src, dst, axis, step):
        return remote(src, dst, arm_send.at[c, k], arm_recv.at[c, k], axis, step)

    arms = [[
        arm(c, 0, box[c].at[3:11, 3:6], box[c].at[3:11, 11:14], "gy", -1),
        arm(c, 1, box[c].at[3:11, 8:11], box[c].at[3:11, 0:3], "gy", 1),
        arm(c, 2, box[c].at[3:6, 3:11], box[c].at[11:14, 3:11], "gx", -1),
        arm(c, 3, box[c].at[8:11, 3:11], box[c].at[0:3, 3:11], "gx", 1),
        arm(c, 4, arm_sd[c], arm_ru[c], "gz", -1),
        arm(c, 5, arm_su[c], arm_rd[c], "gz", 1)] for c in range(GROUPS)]
    arm_axes = ("gy", "gy", "gx", "gx", "gz", "gz")

    for c in range(GROUPS):
        @pl.when(has_high["gz"])
        def _():
            z_copies[c].wait_recv()

        for half in range(2):
            def build(x, packed, c=c, half=half):
                low, high = packed
                parent_tiles = jnp.swapaxes(parent_v[8 * c:8 * c + 8, 4 * half + x], 0, 1)
                lanes_moved = zr[c][half]
                for y in range(8):
                    at = 8 * x + y
                    own = pltpu.roll(moved[c][4 * half + x + s0, y], NZ - s2, 1)
                    beyond = pltpu.roll(lanes_moved, lax.rem(2 * NZ - s2 - 4 * at, NZ), 1)
                    inside = (gx * NX + 4 * half + x + s0 < ex * NX) & (gy * NY + y + s1 < ey * NY)
                    limit = jnp.where(inside, ez * NZ - gz * NZ - s2, 0)
                    tile = jnp.where(lane < NZ - s2, own, beyond)
                    tile = jnp.where(lane < limit, tile, parent_tiles[y])
                    box[c][3 + 4 * half + x, 3 + y] = tile
                    low = jnp.where(group == at, pltpu.roll(tile, 4 * at, 1), low)
                    high = jnp.where(group == at, pltpu.roll(tile, lax.rem(4 * at + 4, NZ), 1), high)
                return low, high
            zero = jnp.zeros((8, NZ), F32)
            low, high = lax.fori_loop(0, 4, build, (zero, zero))
            arm_sd[c][half] = low
            arm_su[c][half] = high

        for k in range(6):
            @pl.when((has_low if k % 2 == 0 else has_high)[arm_axes[k]])
            def _():
                arms[c][k].start()

    for c in range(GROUPS):
        for k in range(6):
            @pl.when((has_high if k % 2 == 0 else has_low)[arm_axes[k]])
            def _():
                arms[c][k].wait_recv()

        def line(m3, m2, m1, u0, p1, p2, p3):
            d1, d2 = p1 - m1, p2 - m2
            t1, t2, t3 = p1 + m1, p2 + m2, p3 + m3
            first = 8.0 * d1 - d2
            second = 16.0 * t1 - t2 - 30.0 * u0
            sixth = t3 - 6.0 * t2 + 15.0 * t1
            return first, second, sixth

        for half in range(2):
            def work(x4, carry, c=c, half=half):
                x = 4 * half + x4
                column = [box[c][3 + x, y] for y in range(14)]
                low_pack, high_pack = arm_rd[c][half], arm_ru[c][half]
                for y in range(8):
                    at = 8 * x4 + y
                    u0 = column[3 + y]
                    ends = jnp.where(lane < 64, pltpu.roll(high_pack, lax.rem(NZ - 4 * at, NZ), 1),
                                     pltpu.roll(low_pack, lax.rem(2 * NZ - 4 - 4 * at, NZ), 1))
                    taps = []
                    for o in (3, 2, 1):
                        taps.append(pltpu.roll(jnp.where(lane >= NZ - o, ends, u0), o, 1))
                    taps.append(u0)
                    for o in (1, 2, 3):
                        taps.append(pltpu.roll(jnp.where(lane < o, ends, u0), NZ - o, 1))
                    fz, sz, qz = line(*taps)
                    fy, sy, qy = line(*column[y:y + 7])
                    fx, sx, qx = line(*[box[c][x + o, 3 + y] for o in range(3)], u0,
                                      *[box[c][x + o, 3 + y] for o in range(4, 7)])
                    slope_v[8 * c + y, x] = qx + qy + qz - 60.0 * u0
                    full = jnp.concatenate([fx, fy, fz, sx, sy, sz], axis=0)
                    top = full.astype(BF16)
                    mixed[0:48, 128 * y:128 * y + 128] = top
                    mixed[48:96, 128 * y:128 * y + 128] = (full - top.astype(F32)).astype(BF16)
                product = jnp.dot(weights[c], mixed[...], preferred_element_type=F32)
                product = product[0:24] + product[24:48]
                if c == 0:
                    acc[x] = product
                else:
                    acc[x] = acc[x] + product
                return carry
            lax.fori_loop(0, 4, work, 0)

    stores = []
    for ref, hbm, k in ((slope_v, slope_hbm, 0), (value_v, value_hbm, 1)):
        stores.append(pltpu.make_async_copy(ref, hbm, store_sem.at[k]))

    def close(x, carry):
        factors = [1.0 + 0.25 * jnp.tanh(box[0][3 + x, 3 + y][0:1]) for y in range(8)]
        for c in range(GROUPS):
            slopes, values = [], []
            for y in range(8):
                slope = factors[y] * acc[x, 8 * c:8 * c + 8, 128 * y:128 * y + 128] + slope_v[8 * c + y, x] * (1.0 / 64.0)
                slopes.append(slope)
                values.append(box[c][3 + x, 3 + y] + 0.125 * slope)
            slope_v[8 * c:8 * c + 8, x] = jnp.swapaxes(jnp.stack(slopes), 0, 1)
            value_v[8 * c:8 * c + 8, x] = jnp.swapaxes(jnp.stack(values), 0, 1)
        return carry
    lax.fori_loop(0, NX, close, 0)
    for store in stores:
        store.start()

    @pl.when(has_low["gy"])
    def _():
        for c in range(GROUPS):
            for h in range(2):
                a_copies[c][h].wait_send()

    @pl.when(has_low["gx"])
    def _():
        for c in range(GROUPS):
            b_copies[c].wait_send()

    @pl.when(has_low["gz"])
    def _():
        for c in range(GROUPS):
            z_copies[c].wait_send()
    for k in range(6):
        @pl.when((has_low if k % 2 == 0 else has_high)[arm_axes[k]])
        def _():
            for c in range(GROUPS):
                arms[c][k].wait_send()
    for store in stores:
        store.wait()


def local(fields_now, parent, advect, diffuse, box_shift):
    shape = jax.ShapeDtypeStruct(fields_now.shape, F32)
    whole = pltpu.VMEM(fields_now.shape, F32)
    packed = [pltpu.VMEM((2, 8, NZ), F32)] * GROUPS
    dma = pltpu.SemaphoreType.DMA
    scratch = [
        whole, whole, whole, whole,
        pltpu.VMEM((NX, 24, NY * NZ), F32), pltpu.VMEM((96, NY * NZ), BF16),
        pltpu.VMEM((GROUPS, 48, 96), BF16), pltpu.VMEM((24, 96), F32),
        *[pltpu.VMEM((4, 12, 8, NZ), F32)] * (2 * GROUPS),
        *[pltpu.VMEM((12, 8, 8, NZ), F32)] * GROUPS,
        *packed, *packed,
        *[pltpu.VMEM((14, 14, 8, NZ), F32)] * GROUPS,
        *packed, *packed, *packed, *packed,
        dma((GROUPS + 1,)), dma((2,)), dma((GROUPS, 2)), dma((GROUPS, 2)), dma((GROUPS,)), dma((GROUPS,)),
        dma((GROUPS,)), dma((GROUPS,)), dma((GROUPS, 6)), dma((GROUPS, 6)),
    ]
    hbm, vmem = pl.BlockSpec(memory_space=pl.ANY), pl.BlockSpec(memory_space=pltpu.VMEM)
    return pl.pallas_call(
        kernel,
        out_shape=(shape, shape),
        in_specs=[pl.BlockSpec(memory_space=pltpu.SMEM), hbm, hbm, vmem, vmem],
        out_specs=(hbm, hbm),
        scratch_shapes=scratch,
        compiler_params=pltpu.CompilerParams(collective_id=0, has_side_effects=True),
        name="section",
    )(box_shift, fields_now, parent, advect, diffuse)


def solution(mesh):
    return jax.shard_map(
        local,
        mesh=mesh,
        in_specs=(P(None, "gx", "gy", "gz"), P(None, "gx", "gy", "gz"), P(), P(), P()),
        out_specs=(P(None, "gx", "gy", "gz"), P(None, "gx", "gy", "gz")),
        check_vma=False,
    )
```

time: 103 us -> 46.2 us (0.45)
  the two profiles are of different devices: /device:TPU:111 before, /device:TPU:99 now
where the time goes in v1:
time: 46.2 us; the launch traced here: 46 us
  Pallas kernels  42.3 us (92%)
  local copies, waits for them, and re-layouts  3.04 us (7%)
  between operations  0.65 us (1%)
    pallas_call x1, Pallas kernels, local(): pl.pallas_call(kernel, out_shape=(shape, shape), in_specs=[pl.BlockSpec(m...  42.3 us
    unnamed x4, local copies, waits for them, and re-layouts  3.04 us

profile of v1, /device:TPU:99, one launch (start us, length us, event | category | flops | bytes accessed | tf_op | source)
XLA Modules:
  0.0 46.0 jit_solution(16550265490769092805)
XLA Ops:
  0.6 42.3 %section.1 = (f32[24,8,8,128]{3,2,1,0:T(8,128)}, f32[24,8,8,128]{3,2,1,0:T(8,128)}) custom-call(s32[3]{0:T(128)} %shift.1, f32[24,8,8,128]{3,2,1,0:T(8,128)} %now_hbm.1, f32[24,8,8,128]{3,2,1,0:T(8,128)} %parent_hbm.1, f32[3,24,24]{2,1,0:T(8,128)} %advect.1, f32[3,24,24]{2,1,0:T(8,128)} %diffuse.1), custom_call_target="tpu_custom_call" | custom-call | tf_op jit(solution)/shard_map/section/pallas_call | solution.py:307
  43.0 0.0 copy-start
  43.0 2.2 %copy.9 = f32[24,8,8,128]{3,2,1,0:T(8,128)} copy(f32[24,8,8,128]{3,2,1,0:T(8,128)} %get-tuple-element.4) | data formatting | bytes 1572864
  45.1 0.0 copy-done
  45.2 0.9 %copy.10 = f32[24,8,8,128]{3,2,1,0:T(8,128)} copy(f32[24,8,8,128]{3,2,1,0:T(8,128)S(1)} %copy-done) | data formatting | bytes 1572864
Async XLA Ops:
  43.0 2.2 %copy-start = (f32[24,8,8,128]{3,2,1,0:T(8,128)S(1)}, f32[24,8,8,128]{3,2,1,0:T(8,128)}, u32[]{:S(2)}) copy-start(f32[24,8,8,128]{3,2,1,0:T(8,128)} %get-tuple-element.5) | copy-start | bytes 2359300
